TPU v7x, 32 devices: a whole 2x2x4 slice. The times are simulated.
32 devices in a mesh: dp: 8 (over y, x, core), expert: 4 (over z).
Axes of the slice: x: 2, y: 2, z: 4, core: 2. Of those that a mesh axis runs over, the one named last changes fastest.
Arguments:
- tokens: bfloat16 [4096, 2048], P(('dp', 'expert')), may hold values from -6 to 6
- routes: int32 [4096, 2], P(('dp', 'expert')), may hold values from 0 to 3, as said below
- grad_hidden: bfloat16 [4096, 2, 768], P(('dp', 'expert')), may hold values from -1.1953125 to 1.1953125
- w_gate: bfloat16 [4, 2048, 768], P('expert'), may hold values from -0.125 to 0.125
- w_up: bfloat16 [4, 2048, 768], P('expert'), may hold values from -0.125 to 0.125
Outputs:
- grad_tokens: bfloat16 [4096, 2048], P(('dp', 'expert'))
- grad_gate: float32 [4, 2048, 768], P('expert', 'dp')
- grad_up: float32 [4, 2048, 768], P('expert', 'dp')
Inputs may be any that keep to these rules, and one draw needn't show every extreme that they name: `routes`: each row names 2 different experts. In each data group 2 experts are hot, the same for all rows of the group: in the rows of one device each hot expert of its group is named more often than every other expert and at most 73 times, every other expert at most 64 times. In the rows of every device some expert is named exactly 64 times; in the rows of some device a hot expert is named exactly 73 times. Every expert is hot in some data group. The indices of a group's two hot experts never differ by 2.
All inputs are finite; a program needn't handle non-finite values.
Results may differ from a plain program's by a relative error of at most 0.012.
Values may be sent and summed in bfloat16 or wider, within the bound.
A program may use at most 128 MiB of HBM per device.

v0:
```python
import jax
import jax.numpy as jnp
from jax import lax
from jax.sharding import PartitionSpec as P


def expert_grads(rows_x, rows_dh, gate_w, up_w):
    gate_act = jnp.dot(rows_x, gate_w, preferred_element_type=jnp.float32)
    up_act = jnp.dot(rows_x, up_w, preferred_element_type=jnp.float32)
    gate_sig = jax.nn.sigmoid(gate_act)
    grad_wide = rows_dh.astype(jnp.float32)
    gate_delta = (grad_wide * up_act * gate_sig * (1.0 + gate_act * (1.0 - gate_sig))).astype(
        jnp.bfloat16
    )
    up_delta = (grad_wide * gate_act * gate_sig).astype(jnp.bfloat16)
    back_rows = lax.dot_general(
        gate_delta, gate_w, (((1,), (1,)), ((), ())), preferred_element_type=jnp.float32
    )
    back_rows = back_rows + lax.dot_general(
        up_delta, up_w, (((1,), (1,)), ((), ())), preferred_element_type=jnp.float32
    )
    gate_grad = lax.dot_general(
        rows_x, gate_delta, (((0,), (0,)), ((), ())), preferred_element_type=jnp.float32
    )
    up_grad = lax.dot_general(
        rows_x, up_delta, (((0,), (0,)), ((), ())), preferred_element_type=jnp.float32
    )
    return (back_rows.astype(jnp.bfloat16), gate_grad, up_grad)


def tile_grads(got_rows, got_grads, begin, finish, gate_w, up_w):
    groups = got_rows.shape[0]
    width = finish - begin
    rows_x = got_rows[:, begin:finish].reshape(groups * width, got_rows.shape[2])
    rows_dh = got_grads[:, begin:finish].reshape(groups * width, got_grads.shape[2])
    back_rows, gate_grad, up_grad = expert_grads(rows_x, rows_dh, gate_w, up_w)
    return (back_rows.reshape(groups, width, got_rows.shape[2]), gate_grad, up_grad)


def per_device(tokens, routes, grad_hidden, w_gate, w_up):
    tok_rows, features = tokens.shape
    per_token = routes.shape[1]
    hidden = w_gate.shape[2]
    groups = lax.axis_size("expert")
    pair_count = tok_rows * per_token
    cold_most = per_token * tok_rows // groups
    cold_floor = cold_most - 2 - cold_most // 8
    hot_total = pair_count - (groups - 3) * cold_floor - cold_most
    hot_most = (hot_total + 1) // 2 + min((hot_total - 2 * cold_most - 2) // 2, cold_most // 4)
    chosen = routes.reshape(pair_count)
    expert_ids = jnp.arange(groups, dtype=jnp.int32)
    member = (chosen[:, None] == expert_ids[None, :]).astype(jnp.int32)
    ranked = jnp.sum(jnp.cumsum(member, axis=0) * member, axis=1) - 1
    own_gate = w_gate[0]
    own_up = w_up[0]
    second_part = (hot_most - cold_most + 1) // 2
    limit = cold_most + second_part
    position = chosen * hot_most + ranked
    send_rows = (
        jnp.zeros((groups * hot_most, features), jnp.bfloat16)
        .at[position]
        .set(jnp.repeat(tokens, per_token, axis=0))
    )
    send_grads = (
        jnp.zeros((groups * hot_most, hidden), jnp.bfloat16)
        .at[position]
        .set(grad_hidden.reshape(pair_count, hidden))
    )
    got_rows, got_grads = (
        lax.all_to_all(
            send_rows.reshape(groups, hot_most, features),
            "expert",
            split_axis=0,
            concat_axis=0,
            tiled=True,
        ),
        lax.all_to_all(
            send_grads.reshape(groups, hot_most, hidden),
            "expert",
            split_axis=0,
            concat_axis=0,
            tiled=True,
        ),
    )
    head_back, main_gate, main_up = tile_grads(got_rows, got_grads, 0, limit, own_gate, own_up)
    tail_back, extra_gate, extra_up = tile_grads(
        got_rows, got_grads, limit, hot_most, own_gate, own_up
    )
    back_tiles = jnp.concatenate([head_back, tail_back], axis=1)
    returned = lax.all_to_all(back_tiles, "expert", split_axis=0, concat_axis=0, tiled=True)
    pair_back = returned.reshape(groups * hot_most, features)[position]
    grad_tokens = jnp.sum(
        pair_back.reshape(tok_rows, per_token, features).astype(jnp.float32), axis=1
    ).astype(jnp.bfloat16)
    kept_gate, spill_gate, kept_up, spill_up = (
        lax.psum_scatter(
            main_gate.astype(jnp.bfloat16), "dp", scatter_dimension=0, tiled=True
        ).astype(jnp.float32),
        lax.psum_scatter(
            extra_gate.astype(jnp.bfloat16), "dp", scatter_dimension=0, tiled=True
        ).astype(jnp.float32),
        lax.psum_scatter(
            main_up.astype(jnp.bfloat16), "dp", scatter_dimension=0, tiled=True
        ).astype(jnp.float32),
        lax.psum_scatter(
            extra_up.astype(jnp.bfloat16), "dp", scatter_dimension=0, tiled=True
        ).astype(jnp.float32),
    )
    gate_part = kept_gate + spill_gate
    up_part = kept_up + spill_up
    return (grad_tokens, gate_part[None], up_part[None])


def solution(mesh):
    placed = (
        P(("dp", "expert"), None),
        P(("dp", "expert"), None),
        P(("dp", "expert"), None, None),
        P("expert", None, None),
        P("expert", None, None),
    )
    return jax.shard_map(
        per_device,
        mesh=mesh,
        in_specs=placed,
        out_specs=(P(("dp", "expert"), None), P("expert", "dp", None), P("expert", "dp", None)),
        check_vma=False,
    )
```

profile of v0, /device:TPU:10, one launch (start us, length us, event | category | flops | bytes accessed | tf_op | source)
XLA Modules:
  0.0 285.6 jit_solution(9467000575477504466)
XLA Ops:
  12.3 2.4 scatter_custom_fusion
  16.6 5.3 %all-to-all-start = ((bf16[4,73,768]{2,1,0:T(8,128)(2,1)}), bf16[4,73,768]{2,1,0:T(8,128)(2,1)}, u32[]{:S(2)}, u32[]{:S(2)}) async-start(bf16[4,73,768]{2,1,0:T(8,128)(2,1)} %reshape.95), calls=%async_computation | async-start | bytes 983040 | tf_op jit(solution)/shard_map/all_to_all | solution.py:77
  21.9 2.7 broadcast_in_dim.21
  24.6 2.3 reshape.126
  26.9 3.9 %scatter_custom_fusion.1 = bf16[292,2048]{1,0:T(8,128)(2,1)} fusion(s32[256]{0:T(256)S(1)} %bitcast.86, bf16[256,2048]{1,0:T(8,128)(2,1)} %reshape.126, bf16[]{:T(256)} %constant.6.clone.1), kind=kCustom, calls=%fused_computation.40 | custom fusion | bytes 1196544 | tf_op jit(solution)/shard_map/scatter | solution.py:62
  30.8 2.7 reshape.97
  33.5 6.6 %all-to-all-start.1 = ((bf16[4,73,2048]{2,1,0:T(8,128)(2,1)}), bf16[4,73,2048]{2,1,0:T(8,128)(2,1)}, u32[]{:S(2)}, u32[]{:S(2)}) async-start(bf16[4,73,2048]{2,1,0:T(8,128)(2,1)} %reshape.97), calls=%async_computation.1 | async-start | bytes 2621440 | tf_op jit(solution)/shard_map/all_to_all | solution.py:70
  42.1 2.2 reshape.104
  44.3 23.4 %all-to-all-done.1 = bf16[4,73,2048]{2,1,0:T(8,128)(2,1)} async-done(((bf16[4,73,2048]{2,1,0:T(8,128)(2,1)}), bf16[4,73,2048]{2,1,0:T(8,128)(2,1)}, u32[]{:S(2)}, u32[]{:S(2)}) %all-to-all-start.1) | async-done | bytes 1196064 | tf_op jit(solution)/shard_map/all_to_all | solution.py:70
  67.7 2.4 slice.28
  70.1 2.6 reshape.98
  72.7 3.6 %multiply_convert_fusion = (bf16[276,768]{1,0:T(8,128)(2,1)S(1)}, f32[276,768]{1,0:T(8,128)}) fusion(f32[276,768]{1,0:T(8,128)} %reshape.104, bf16[276,2048]{1,0:T(8,128)(2,1)} %reshape.98, bf16[1,2048,768]{2,1,0:T(8,128)(2,1)S(1)} %copy-done), kind=kOutput, calls=%fused_computation.36 | convolution fusion | flops 869492736 | bytes 6395904 | tf_op jit(solution)/shard_map/dot_general | solution.py:8
  77.1 3.5 %convolution_convert_fusion.1 = bf16[2048,768]{1,0:T(8,128)(2,1)} fusion(bf16[276,2048]{1,0:T(8,128)(2,1)S(1)} %copy-done.3, bf16[276,768]{1,0:T(8,128)(2,1)S(1)} %get-tuple-element.5), kind=kOutput, calls=%fused_computation.4 | convolution fusion | flops 869793792 | bytes 4700160 | tf_op jit(solution)/shard_map/dot_general | solution.py:25
  83.2 2.7 convolution_convert_fusion
  86.2 4.2 %fusion.37 = bf16[276,768]{1,0:T(8,128)(2,1)S(1)} fusion(f32[276,768]{1,0:T(8,128)} %reshape.104, bf16[276,2048]{1,0:T(8,128)(2,1)} %reshape.98, bf16[1,2048,768]{2,1,0:T(8,128)(2,1)} %param.9, f32[276,768]{1,0:T(8,128)} %get-tuple-element.6), kind=kOutput, calls=%fused_computation.31 | convolution fusion | flops 870340608 | bytes 6395904 | tf_op jit(solution)/shard_map/dot_general | solution.py:9
  91.2 3.6 %convolution_convert_fusion.3 = bf16[2048,768]{1,0:T(8,128)(2,1)} fusion(bf16[276,2048]{1,0:T(8,128)(2,1)S(1)} %copy-done.4, bf16[276,768]{1,0:T(8,128)(2,1)S(1)} %fusion.37), kind=kOutput, calls=%fused_computation.6 | convolution fusion | flops 869793792 | bytes 4700160 | tf_op jit(solution)/shard_map/dot_general | solution.py:22
  94.8 2.5 fusion.49
  97.3 2.7 convolution_convert_fusion.2
  102.9 2.2 fusion.4
  105.3 2.1 fusion.19
  107.5 2.6 reshape.99
  110.1 2.6 pad_maximum_fusion
  112.7 7.9 %all-to-all-start.2 = ((bf16[4,73,2048]{2,1,0:T(8,128)(2,1)}), bf16[4,73,2048]{2,1,0:T(8,128)(2,1)}, u32[]{:S(2)}, u32[]{:S(2)}) async-start(bf16[4,73,2048]{2,1,0:T(8,128)(2,1)} %pad_maximum_fusion), calls=%async_computation.2 | async-start | bytes 2621440 | tf_op jit(solution)/shard_map/all_to_all | solution.py:90
  120.6 27.2 %all-to-all-done.2 = bf16[4,73,2048]{2,1,0:T(8,128)(2,1)} async-done(((bf16[4,73,2048]{2,1,0:T(8,128)(2,1)}), bf16[4,73,2048]{2,1,0:T(8,128)(2,1)}, u32[]{:S(2)}, u32[]{:S(2)}) %all-to-all-start.2) | async-done | bytes 1196064 | tf_op jit(solution)/shard_map/all_to_all | solution.py:90
  147.7 2.7 reshape.102
  150.4 4.8 %gather_fusion = bf16[256,2048]{1,0:T(8,128)(2,1)} fusion(bf16[292,2048]{1,0:T(8,128)(2,1)} %reshape.102, s32[1024]{0:T(1024)S(1)} %pad_clamp_fusion), kind=kCustom, calls=%fused_computation | custom fusion | bytes 2098176 | tf_op jit(solution)/shard_map/gather | solution.py:91
  155.2 2.5 reshape.103
  157.8 4.6 %reduce_sum.22 = bf16[128,2048]{1,0:T(8,128)(2,1)} reduce(bf16[128,2,2048]{2,1,0:T(2,128)(2,1)} %reshape.103, bf16[]{:T(256)} %constant.6.clone.1), dimensions={1}, to_apply=%region_5.6 | reduce | flops 262144 | bytes 1572866 | tf_op jit(solution)/shard_map/reduce_sum | solution.py:92
  162.3 15.9 %reduce-scatter.11.cloned.1.call-done = bf16[256,768]{1,0:T(8,128)(2,1)} async-done(((bf16[2048,768]{1,0:T(8,128)(2,1)}), bf16[256,768]{1,0:T(8,128)(2,1)}) %reduce-scatter.11.cloned.1.call-update) | async-done | bytes 393232 | tf_op jit(solution)/shard_map/reduce_scatter | solution.py:105
  180.3 47.4 %reduce-scatter.5.cloned.1.call-done = bf16[256,768]{1,0:T(8,128)(2,1)} async-done(((bf16[2048,768]{1,0:T(8,128)(2,1)}), bf16[256,768]{1,0:T(8,128)(2,1)}) %reduce-scatter.5.cloned.1.call-update) | async-done | bytes 393232 | tf_op jit(solution)/shard_map/reduce_scatter | solution.py:96
  227.7 49.3 %reduce-scatter.7.cloned.1.call-done = bf16[256,768]{1,0:T(8,128)(2,1)} async-done(((bf16[2048,768]{1,0:T(8,128)(2,1)}), bf16[256,768]{1,0:T(8,128)(2,1)}) %reduce-scatter.7.cloned.1.call-update) | async-done | bytes 393232 | tf_op jit(solution)/shard_map/reduce_scatter | solution.py:99
  277.0 2.1 add_bitcast_fusion.1
  (56 shorter events, 18.5 us)
Async XLA Ops:
  7.2 65.5 %copy-start = (bf16[1,2048,768]{2,1,0:T(8,128)(2,1)S(1)}, bf16[1,2048,768]{2,1,0:T(8,128)(2,1)}, u32[]{:S(2)}) copy-start(bf16[1,2048,768]{2,1,0:T(8,128)(2,1)} %param.8) | copy-start | bytes 9437188
  16.6 16.9 %all-to-all-start = ((bf16[4,73,768]{2,1,0:T(8,128)(2,1)}), bf16[4,73,768]{2,1,0:T(8,128)(2,1)}, u32[]{:S(2)}, u32[]{:S(2)}) async-start(bf16[4,73,768]{2,1,0:T(8,128)(2,1)} %reshape.95), calls=%async_computation | async-start | bytes 983040 | tf_op jit(solution)/shard_map/all_to_all | solution.py:77
  33.5 34.2 %all-to-all-start.1 = ((bf16[4,73,2048]{2,1,0:T(8,128)(2,1)}), bf16[4,73,2048]{2,1,0:T(8,128)(2,1)}, u32[]{:S(2)}, u32[]{:S(2)}) async-start(bf16[4,73,2048]{2,1,0:T(8,128)(2,1)} %reshape.97), calls=%async_computation.1 | async-start | bytes 2621440 | tf_op jit(solution)/shard_map/all_to_all | solution.py:70
  40.1 122.3 %reduce-scatter.9.cloned.1.call-start = ((), (), s32[]{:S(2)}) async-start(), calls=%async_computation.9 | async-start | bytes 3538944 | tf_op jit(solution)/shard_map/reduce_scatter | solution.py:102
  72.7 4.4 %copy-start.3 = (bf16[276,2048]{1,0:T(8,128)(2,1)S(1)}, bf16[276,2048]{1,0:T(8,128)(2,1)}, u32[]{:S(2)}) copy-start(bf16[276,2048]{1,0:T(8,128)(2,1)} %reshape.98) | copy-start | bytes 3391492
  76.3 0.8 copy-start.6
  80.6 97.6 %reduce-scatter.11.cloned.1.call-start = ((), (), s32[]{:S(2)}) async-start(), calls=%async_computation.10 | async-start | bytes 3538944 | tf_op jit(solution)/shard_map/reduce_scatter | solution.py:105
  86.0 141.7 %reduce-scatter.5.cloned.1.call-start = ((), (), s32[]{:S(2)}) async-start(), calls=%async_computation.7 | async-start | bytes 3538944 | tf_op jit(solution)/shard_map/reduce_scatter | solution.py:96
  86.2 5.0 %copy-start.4 = (bf16[276,2048]{1,0:T(8,128)(2,1)S(1)}, bf16[276,2048]{1,0:T(8,128)(2,1)}, u32[]{:S(2)}) copy-start(bf16[276,2048]{1,0:T(8,128)(2,1)} %reshape.98) | copy-start | bytes 3391492
  90.4 0.8 copy-start.5
  94.8 182.3 %reduce-scatter.7.cloned.1.call-start = ((), (), s32[]{:S(2)}) async-start(), calls=%async_computation.8 | async-start | bytes 3538944 | tf_op jit(solution)/shard_map/reduce_scatter | solution.py:99
  100.0 1.9 copy-start.1
  102.9 2.3 copy-start.2
  102.9 2.4 copy-start.7
  112.7 35.1 %all-to-all-start.2 = ((bf16[4,73,2048]{2,1,0:T(8,128)(2,1)}), bf16[4,73,2048]{2,1,0:T(8,128)(2,1)}, u32[]{:S(2)}, u32[]{:S(2)}) async-start(bf16[4,73,2048]{2,1,0:T(8,128)(2,1)} %pad_maximum_fusion), calls=%async_computation.2 | async-start | bytes 2621440 | tf_op jit(solution)/shard_map/all_to_all | solution.py:90
Sparse Core Ops, SparseCore 0:
  80.8 47.9 reduce-scatter.8
  132.1 46.0 reduce-scatter.10
  181.6 46.0 reduce-scatter.4
  230.9 46.0 reduce-scatter.6
where the time goes:
time: 288 us; the launch traced here: 286 us
  waiting for transfers between devices  163 us (57%)
  local copies, waits for them, and re-layouts  42.4 us (15%)
  matrix products  29.6 us (10%)
  starting transfers between devices  20.1 us (7%)
  other arithmetic  16.4 us (6%)
  between operations  13.9 us (5%)
    reduce_scatter x1, waiting for transfers between devices, per_device(): lax.psum_scatter(extra_gate.astype(jnp.bfloat16), 'dp', scatter_dimension...  49.3 us
    reduce_scatter x1, waiting for transfers between devices, per_device(): lax.psum_scatter(main_gate.astype(jnp.bfloat16), 'dp', scatter_dimension=...  47.4 us
    all_to_all x1, waiting for transfers between devices, per_device(): lax.all_to_all(back_tiles, 'expert', split_axis=0, concat_axis=0, tiled=T...  27.2 us
    all_to_all x1, waiting for transfers between devices, per_device(): lax.all_to_all(send_rows.reshape(groups, hot_most, features), 'expert', s...  23.4 us
    reduce_scatter x1, waiting for transfers between devices, per_device(): lax.psum_scatter(extra_up.astype(jnp.bfloat16), 'dp', scatter_dimension=0...  15.9 us
    all_to_all x1, starting transfers between devices, per_device(): lax.all_to_all(back_tiles, 'expert', split_axis=0, concat_axis=0, tiled=T...  7.89 us
    dot_general x2, matrix products, expert_grads(): up_act = jnp.dot(rows_x, up_w, preferred_element_type=jnp.float32)  6.72 us
    all_to_all x1, starting transfers between devices, per_device(): lax.all_to_all(send_rows.reshape(groups, hot_most, features), 'expert', s...  6.57 us
  transfers between devices with their start and end apart: 7, of which 5 were waited for; matrix products, arithmetic and copies ran while one was open for 22% of the time, Pallas kernels for 0%

commit v1 on v0

v1 whole, which is shorter than its diff:
```python
import functools

import jax
import jax.numpy as jnp
from jax import lax
from jax.experimental import pallas as pl
from jax.experimental.pallas import tpu as pltpu
from jax.sharding import PartitionSpec as P

MESH = pl.DeviceIdType.MESH
BF = jnp.bfloat16
F32 = jnp.float32


def dot(a, b, da, db):
    return lax.dot_general(a, b, (((da,), (db,)), ((), ())), preferred_element_type=F32)


def rs_plan(bits):
    orders = (tuple(range(bits)), (0,) + tuple(range(bits - 1, 0, -1)))
    index = {}
    for which, order in enumerate(orders):
        done = 1
        for bit in order[1:]:
            flag = 1 << bit
            for mask in range(1 << bits):
                if mask & done or mask & flag:
                    continue
                index[which, bit, mask] = len(index)
            done |= flag
    return orders, index


def kernel(
    groups, ways, cap, tok_ref, rt_ref, gh0_ref, gh1_ref, wg_hbm, wu_hbm,
    out_tok, out_gate, out_up,
    wg, wu, pick, send, rows, delta, back, ret, core_send, core_recv, hop_send, hop_recv, acc,
    w_sem, z_ssem, z_rsem, b_ssem, b_rsem, c_ssem, c_rsem, h_ssem, h_rsem,
):
    features = tok_ref.shape[1]
    toks = tok_ref.shape[0]
    hidden = gh0_ref.shape[1]
    block = features // ways
    bits = ways.bit_length() - 1
    orders, index = rs_plan(bits)
    me = lax.axis_index("expert")
    dp = lax.axis_index("dp")
    my_bits = [lax.rem(dp // (1 << b), 2) for b in range(bits)]

    def peer_dp(mask):
        total = 0
        for b in range(bits):
            bit = 1 - my_bits[b] if mask >> b & 1 else my_bits[b]
            total = total + bit * (1 << b)
        return total

    load_g = pltpu.make_async_copy(wg_hbm, wg, w_sem.at[0])
    load_u = pltpu.make_async_copy(wu_hbm, wu, w_sem.at[1])
    load_g.start()
    load_u.start()

    barrier = pltpu.get_barrier_semaphore()
    for off in range(1, groups):
        pl.semaphore_signal(
            barrier, inc=1, device_id={"expert": lax.rem(me + off, groups)}, device_id_type=MESH
        )
    for b in range(bits):
        pl.semaphore_signal(
            barrier, inc=1, device_id={"dp": peer_dp(1 << b)}, device_id_type=MESH
        )

    r0 = rt_ref[0:1, :]
    r1 = rt_ref[1:2, :]
    wide = max(groups, 8)
    ids = lax.broadcasted_iota(jnp.int32, (wide, toks), 0)
    is0 = (ids == r0).astype(F32)
    is1 = (ids == r1).astype(F32)
    before = (
        lax.broadcasted_iota(jnp.int32, (toks, toks), 0)
        < lax.broadcasted_iota(jnp.int32, (toks, toks), 1)
    ).astype(F32).astype(BF)
    earlier = dot((is0 + is1).astype(BF), before, 1, 0)
    pos0 = r0.astype(F32) * cap + jnp.sum(is0 * earlier, axis=0, keepdims=True)
    pos1 = r1.astype(F32) * cap + jnp.sum(is1 * earlier, axis=0, keepdims=True)
    slot = lax.broadcasted_iota(jnp.int32, (groups * cap, toks), 0).astype(F32)
    m0 = (slot == pos0).astype(F32)
    m1 = (slot == pos1).astype(F32)
    pick[...] = (m0 + m1).astype(BF)
    send[:, features:] = (
        dot(m0.astype(BF), gh0_ref[...], 1, 0) + dot(m1.astype(BF), gh1_ref[...], 1, 0)
    ).astype(BF)
    step = 512
    for c in range(0, features, step):
        send[:, c : c + step] = dot(pick[...], tok_ref[:, c : c + step], 1, 0).astype(BF)

    pl.semaphore_wait(barrier, groups - 1 + bits)

    def span(i):
        return pl.ds(pl.multiple_of(i * cap, cap), cap)

    def exchange(src, dst, ssem, rsem):
        sends, recvs = [], []
        for off in range(1, groups):
            to = lax.rem(me + off, groups)
            frm = lax.rem(me + groups - off, groups)
            sends.append(pltpu.make_async_remote_copy(
                src_ref=src.at[span(to)], dst_ref=dst.at[span(me)],
                send_sem=ssem.at[off], recv_sem=rsem.at[off],
                device_id={"expert": to}, device_id_type=MESH))
            recvs.append(pltpu.make_async_remote_copy(
                src_ref=src.at[span(frm)], dst_ref=dst.at[span(frm)],
                send_sem=ssem.at[off], recv_sem=rsem.at[off],
                device_id={"expert": frm}, device_id_type=MESH))
        for copy in sends:
            copy.start()
        return sends, recvs

    out_sends, out_recvs = exchange(send, rows, z_ssem, z_rsem)
    rows[span(me), :] = send[span(me), :]
    load_g.wait()
    load_u.wait()
    for copy in out_recvs:
        copy.wait_recv()

    tile = 256

    def forward(f, carry):
        cols = pl.ds(pl.multiple_of(f * tile, tile), tile)
        ucols = pl.ds(pl.multiple_of(f * tile + hidden, tile), tile)
        dcols = pl.ds(pl.multiple_of(f * tile + features, tile), tile)
        x = rows[:, 0:features]
        gate = dot(x, wg[:, cols], 1, 0)
        up = dot(x, wu[:, cols], 1, 0)
        sig = jax.nn.sigmoid(gate)
        grad = rows[:, dcols].astype(F32)
        delta[:, cols] = (grad * up * sig * (1.0 + gate * (1.0 - sig))).astype(BF)
        delta[:, ucols] = (grad * gate * sig).astype(BF)
        return carry

    lax.fori_loop(0, hidden // tile, forward, 0)

    def weight_block(mask):
        start = pl.multiple_of(peer_dp(mask) * block, block)
        return dot(rows[:, pl.ds(start, block)], delta[...], 0, 0)

    core_sends = {}
    for mask in range(ways - 1, 0, -2):
        place = mask >> 1
        core_send[place] = weight_block(mask).astype(BF)
        copy = pltpu.make_async_remote_copy(
            src_ref=core_send.at[place], dst_ref=core_recv.at[place],
            send_sem=c_ssem.at[place], recv_sem=c_rsem.at[place],
            device_id={"dp": peer_dp(1)}, device_id_type=MESH)
        copy.start()
        core_sends[place] = copy

    def backward(d, carry):
        cols = pl.ds(pl.multiple_of(d * tile, tile), tile)
        back[:, cols] = (
            dot(delta[:, 0:hidden], wg[cols, :], 1, 1)
            + dot(delta[:, hidden:], wu[cols, :], 1, 1)
        ).astype(BF)
        return carry

    lax.fori_loop(0, features // tile, backward, 0)
    back_sends, back_recvs = exchange(back, ret, b_ssem, b_rsem)
    ret[span(me), :] = back[span(me), :]

    hop_sends = []

    def hop(which, bit, mask, value):
        at = index[which, bit, mask ^ (1 << bit)]
        hop_send[at] = value.astype(BF)
        copy = pltpu.make_async_remote_copy(
            src_ref=hop_send.at[at], dst_ref=hop_recv.at[at],
            send_sem=h_ssem.at[at], recv_sem=h_rsem.at[at],
            device_id={"dp": peer_dp(1 << bit)}, device_id_type=MESH)
        copy.start()
        hop_sends.append(copy)

    def arrived(which, bit, mask):
        at = index[which, bit, mask]
        pltpu.make_async_remote_copy(
            src_ref=hop_send.at[at], dst_ref=hop_recv.at[at],
            send_sem=h_ssem.at[at], recv_sem=h_rsem.at[at],
            device_id={"dp": peer_dp(1 << bit)}, device_id_type=MESH).wait_recv()
        return hop_recv[at].astype(F32)

    for mask in range(ways - 2, -1, -2):
        place = mask >> 1
        core_sends[place].wait_recv()
        total = weight_block(mask) + core_recv[place].astype(F32)
        for which in range(2):
            part = total[:, which * hidden : (which + 1) * hidden]
            bit = orders[which][1]
            if mask >> bit & 1:
                hop(which, bit, mask, part)
            else:
                acc[which, place] = part

    for level in range(2, bits):
        for mask in range(ways - 2, -1, -2):
            for which in range(2):
                order = orders[which]
                fixed = sum(1 << b for b in order[:level])
                if mask & fixed:
                    continue
                value = acc[which, mask >> 1] + arrived(which, order[level - 1], mask)
                if mask >> order[level] & 1:
                    hop(which, order[level], mask, value)
                else:
                    acc[which, mask >> 1] = value

    for copy in back_recvs:
        copy.wait_recv()
    for c in range(0, features, step):
        out_tok[:, c : c + step] = dot(pick[...], ret[:, c : c + step], 0, 0).astype(BF)
    out_gate[...] = acc[0, 0] + arrived(0, orders[0][-1], 0)
    out_up[...] = acc[1, 0] + arrived(1, orders[1][-1], 0)

    for copy in out_sends + back_sends + list(core_sends.values()) + hop_sends:
        copy.wait_send()


def per_device(tokens, routes, grad_hidden, w_gate, w_up):
    tok_rows, features = tokens.shape
    per_token = routes.shape[1]
    hidden = w_gate.shape[2]
    groups = lax.axis_size("expert")
    ways = lax.axis_size("dp")
    pair_count = tok_rows * per_token
    cold_most = pair_count // groups
    cold_floor = cold_most - 2 - cold_most // 8
    hot_total = pair_count - (groups - 3) * cold_floor - cold_most
    hot_most = (hot_total + 1) // 2 + min((hot_total - 2 * cold_most - 2) // 2, cold_most // 4)
    cap = (max(hot_most, cold_most) + 15) // 16 * 16
    slots = groups * cap
    block = features // ways
    bits = ways.bit_length() - 1
    hops = len(rs_plan(bits)[1])
    half = ways // 2
    vmem = pl.BlockSpec(memory_space=pltpu.VMEM)
    hbm = pl.BlockSpec(memory_space=pl.ANY)
    dma = pltpu.SemaphoreType.DMA
    tok_grad, gate_grad, up_grad = pl.pallas_call(
        functools.partial(kernel, groups, ways, cap),
        out_shape=(
            jax.ShapeDtypeStruct((tok_rows, features), BF),
            jax.ShapeDtypeStruct((block, hidden), F32),
            jax.ShapeDtypeStruct((block, hidden), F32),
        ),
        in_specs=[vmem, vmem, vmem, vmem, hbm, hbm],
        out_specs=(vmem, vmem, vmem),
        scratch_shapes=[
            pltpu.VMEM((features, hidden), BF),
            pltpu.VMEM((features, hidden), BF),
            pltpu.VMEM((slots, tok_rows), BF),
            pltpu.VMEM((slots, features + hidden), BF),
            pltpu.VMEM((slots, features + hidden), BF),
            pltpu.VMEM((slots, 2 * hidden), BF),
            pltpu.VMEM((slots, features), BF),
            pltpu.VMEM((slots, features), BF),
            pltpu.VMEM((half, block, 2 * hidden), BF),
            pltpu.VMEM((half, block, 2 * hidden), BF),
            pltpu.VMEM((hops, block, hidden), BF),
            pltpu.VMEM((hops, block, hidden), BF),
            pltpu.VMEM((2, half, block, hidden), F32),
            dma((2,)),
            dma((groups,)),
            dma((groups,)),
            dma((groups,)),
            dma((groups,)),
            dma((half,)),
            dma((half,)),
            dma((hops,)),
            dma((hops,)),
        ],
        compiler_params=pltpu.CompilerParams(collective_id=0, has_side_effects=True),
    )(tokens, routes.T, grad_hidden[:, 0], grad_hidden[:, 1], w_gate[0], w_up[0])
    return tok_grad, gate_grad[None], up_grad[None]


def solution(mesh):
    placed = (
        P(("dp", "expert"), None),
        P(("dp", "expert"), None),
        P(("dp", "expert"), None, None),
        P("expert", None, None),
        P("expert", None, None),
    )
    return jax.shard_map(
        per_device,
        mesh=mesh,
        in_specs=placed,
        out_specs=(P(("dp", "expert"), None), P("expert", "dp", None), P("expert", "dp", None)),
        check_vma=False,
    )
```

time: 288 us -> 90 us (0.31)
  waiting for transfers between devices: 163 us -> 0 us
  Pallas kernels: 0 us -> 81.6 us
  local copies, waits for them, and re-layouts: 42.4 us -> 7.48 us
  matrix products: 29.6 us -> 0 us
  starting transfers between devices: 20.1 us -> 0 us
  other arithmetic: 16.4 us -> 0 us
  between operations: 13.9 us -> 0.65 us
    reduce_scatter x4 -> x0, waiting for transfers between devices: 113 us -> none  [the longest x1 49.3 us: per_device(): lax.psum_scatter(extra_gate.astype(jnp.bfloat16), 'dp', scatter_dimension...]
    pallas_call x0 -> x1, Pallas kernels: none -> 81.6 us  [per_device(): pl.pallas_call(functools.partial(kernel, groups, ways, cap), out_shape=(j...]
    all_to_all x3 -> x0, waiting for transfers between devices: 50.6 us -> none  [the longest x1 27.2 us: per_device(): lax.all_to_all(back_tiles, 'expert', split_axis=0, concat_axis=0, tiled=T...]
    dot_general x12 -> x0, matrix products: 29.6 us -> none  [the longest x2 6.72 us: expert_grads(): up_act = jnp.dot(rows_x, up_w, preferred_element_type=jnp.float32)]
    all_to_all x3 -> x0, starting transfers between devices: 19.8 us -> none  [the longest x1 7.89 us: per_device(): lax.all_to_all(back_tiles, 'expert', split_axis=0, concat_axis=0, tiled=T...]
    reshape x10 -> x0, local copies, waits for them, and re-layouts: 18.5 us -> none  [the longest x1 2.69 us: per_device(): send_rows.reshape(groups, hot_most, features)]
    scatter x2 -> x0, local copies, waits for them, and re-layouts: 6.31 us -> none  [the longest x1 3.92 us: per_device(): send_rows = jnp.zeros((groups * hot_most, features), jnp.bfloat16).at[pos...]
    gather x1 -> x0, local copies, waits for them, and re-layouts: 4.83 us -> none  [per_device(): pair_back = returned.reshape(groups * hot_most, features)[position]]
  transfers between devices with their start and end apart: 7 -> 0, of which waited for: 5 -> 0; matrix products, arithmetic and copies ran while one was open for 22% -> 0% of each run, Pallas kernels for 0% -> 0%
where the time goes in v1:
time: 90 us; the launch traced here: 89.7 us
  Pallas kernels  81.6 us (91%)
  local copies, waits for them, and re-layouts  7.48 us (8%)
    pallas_call x1, Pallas kernels, per_device(): pl.pallas_call(functools.partial(kernel, groups, ways, cap), out_shape=(j...  81.6 us
    unnamed x5, local copies, waits for them, and re-layouts  4.9 us

profile of v1, /device:TPU:10, one launch (start us, length us, event | category | flops | bytes accessed | tf_op | source)
XLA Modules:
  0.0 89.7 jit_solution(14247878089507294373)
XLA Ops:
  0.6 1.8 %fusion = (bf16[128,1,768]{2,1,0:T(2,128)(2,1)S(1)}, bf16[128,1,768]{2,1,0:T(2,128)(2,1)S(1)}) fusion(bf16[128,2,768]{2,1,0:T(2,128)(2,1)} %param.7), kind=kLoop, calls=%fused_computation.2 | loop fusion | bytes 786432 | tf_op jit(solution)/shard_map/slice | solution.py:279
  2.4 0.8 copy_bitcast_fusion
  3.2 81.6 %shard_map.76 = (bf16[128,2048]{1,0:T(8,128)(2,1)}, f32[256,768]{1,0:T(8,128)}, f32[256,768]{1,0:T(8,128)}) custom-call(bf16[128,2048]{1,0:T(8,128)(2,1)} %tok_ref.1, s32[2,128]{1,0:T(2,128)} %bitcast.13, bf16[128,768]{1,0:T(8,128)(2,1)} %get-tuple-element.12.gh0_ref, bf16[128,768]{1,0:T(8,128)(2,1)} %get-tuple-element.11.gh1_ref, ...), custom_call_target="tpu_custom_call" | custom-call | tf_op jit(solution)/shard_map/pallas_call | solution.py:245
  84.8 0.0 copy-start
  84.8 2.0 %copy.17 = bf16[128,2048]{1,0:T(8,128)(2,1)} copy(bf16[128,2048]{1,0:T(8,128)(2,1)} %get-tuple-element.16) | data formatting | bytes 1048576
  86.8 2.1 %copy.18 = f32[1,256,768]{2,1,0:T(8,128)} copy(f32[1,256,768]{2,1,0:T(8,128)} %bitcast.12) | data formatting | bytes 1572864
  88.8 0.0 copy-done
  88.9 0.9 copy.19
Async XLA Ops:
  84.8 4.0 %copy-start = (f32[256,768]{1,0:T(8,128)S(1)}, f32[256,768]{1,0:T(8,128)}, u32[]{:S(2)}) copy-start(f32[256,768]{1,0:T(8,128)} %get-tuple-element.8) | copy-start | bytes 2359300

commit v2 on v1

v2 whole, which is shorter than its diff:
```python
import functools

import jax
import jax.numpy as jnp
from jax import lax
from jax.experimental import pallas as pl
from jax.experimental.pallas import tpu as pltpu
from jax.sharding import PartitionSpec as P

MESH = pl.DeviceIdType.MESH
BF = jnp.bfloat16
F32 = jnp.float32


def dot(a, b, da, db):
    return lax.dot_general(a, b, (((da,), (db,)), ((), ())), preferred_element_type=F32)


def rs_plan(bits):
    orders = (tuple(range(bits)), (0,) + tuple(range(bits - 1, 0, -1)))
    index = {}
    for which, order in enumerate(orders):
        done = 1
        for bit in order[1:]:
            flag = 1 << bit
            for mask in range(1 << bits):
                if mask & done or mask & flag:
                    continue
                index[which, bit, mask] = len(index)
            done |= flag
    return orders, index


def kernel(
    groups, ways, cap, tile, tok_ref, rt_ref, gh0_ref, gh1_ref, wg_hbm, wu_hbm,
    out_tok, out_gate, out_up,
    wg, wu, pick, send, rows, xt, dsend, drows, delta_g, delta_u, back, ret,
    core_send, core_recv, hop_send, hop_recv, acc,
    w_sem, z_ssem, z_rsem, d_ssem, d_rsem, b_ssem, b_rsem, c_ssem, c_rsem, h_ssem, h_rsem,
):
    features = tok_ref.shape[1]
    toks = tok_ref.shape[0]
    hidden = gh0_ref.shape[1]
    block = features // ways
    slices = hidden // tile
    bits = ways.bit_length() - 1
    orders, index = rs_plan(bits)
    me = lax.axis_index("expert")
    dp = lax.axis_index("dp")
    my_bits = [lax.rem(dp // (1 << b), 2) for b in range(bits)]
    offs = sorted(range(1, groups), key=lambda off: abs(off - groups // 2))

    def peer_dp(mask):
        total = 0
        for b in range(bits):
            bit = 1 - my_bits[b] if mask >> b & 1 else my_bits[b]
            total = total + bit * (1 << b)
        return total

    def span(i):
        return pl.ds(pl.multiple_of(i * cap, cap), cap)

    barrier = pltpu.get_barrier_semaphore()
    for off in range(1, groups):
        pl.semaphore_signal(
            barrier, inc=1, device_id={"expert": lax.rem(me + off, groups)}, device_id_type=MESH
        )
    for b in range(bits):
        pl.semaphore_signal(
            barrier, inc=1, device_id={"dp": peer_dp(1 << b)}, device_id_type=MESH
        )

    r0 = rt_ref[0:1, :]
    r1 = rt_ref[1:2, :]
    wide = max(groups, 8)
    ids = lax.broadcasted_iota(jnp.int32, (wide, toks), 0)
    is0 = (ids == r0).astype(F32)
    is1 = (ids == r1).astype(F32)
    before = (
        lax.broadcasted_iota(jnp.int32, (toks, toks), 0)
        < lax.broadcasted_iota(jnp.int32, (toks, toks), 1)
    ).astype(F32).astype(BF)
    earlier = dot((is0 + is1).astype(BF), before, 1, 0)
    pos0 = r0.astype(F32) * cap + jnp.sum(is0 * earlier, axis=0, keepdims=True)
    pos1 = r1.astype(F32) * cap + jnp.sum(is1 * earlier, axis=0, keepdims=True)
    slot = lax.broadcasted_iota(jnp.int32, (groups * cap, toks), 0).astype(F32)
    m0 = (slot == pos0).astype(F32)
    m1 = (slot == pos1).astype(F32)
    pick[...] = (m0 + m1).astype(BF)

    started = []

    def push(src, dst, ssem, rsem, target):
        copy = pltpu.make_async_remote_copy(
            src_ref=src, dst_ref=dst, send_sem=ssem, recv_sem=rsem,
            device_id=target, device_id_type=MESH)
        copy.start()
        started.append(copy)
        return copy

    def pull(src, dst, ssem, rsem, target):
        pltpu.make_async_remote_copy(
            src_ref=src, dst_ref=dst, send_sem=ssem, recv_sem=rsem,
            device_id=target, device_id_type=MESH).wait_recv()

    step = 512
    ready = False
    for off in offs:
        to = lax.rem(me + off, groups)
        for c in range(0, features, step):
            send[span(to), c : c + step] = dot(
                pick[span(to), :], tok_ref[:, c : c + step], 1, 0
            ).astype(BF)
        if not ready:
            pl.semaphore_wait(barrier, groups - 1 + bits)
            ready = True
        push(send.at[span(to)], rows.at[span(me)], z_ssem.at[off], z_rsem.at[off], {"expert": to})

    for f in range(slices):
        cols = slice(f * tile, (f + 1) * tile)
        dsend[f] = (
            dot(m0.astype(BF), gh0_ref[:, cols], 1, 0)
            + dot(m1.astype(BF), gh1_ref[:, cols], 1, 0)
        ).astype(BF)
        for off in offs:
            to = lax.rem(me + off, groups)
            push(dsend.at[f, span(to)], drows.at[f, span(me)],
                 d_ssem.at[f, off], d_rsem.at[f, off], {"expert": to})
        drows[f, span(me), :] = dsend[f, span(me), :]

    load_g = pltpu.make_async_copy(wg_hbm, wg, w_sem.at[0])
    load_u = pltpu.make_async_copy(wu_hbm, wu, w_sem.at[1])
    load_g.start()
    load_u.start()
    for c in range(0, features, step):
        rows[span(me), c : c + step] = dot(
            pick[span(me), :], tok_ref[:, c : c + step], 1, 0
        ).astype(BF)
    load_g.wait()
    load_u.wait()
    for off in offs:
        frm = lax.rem(me + groups - off, groups)
        pull(send.at[span(frm)], rows.at[span(frm)], z_ssem.at[off], z_rsem.at[off],
             {"expert": frm})

    def flip(d, carry):
        cols = pl.ds(pl.multiple_of(d * 256, 256), 256)
        xt[cols, :] = rows[:, cols].T
        return carry

    def deltas(f):
        cols = slice(f * tile, (f + 1) * tile)
        gate = dot(rows[...], wg[:, cols], 1, 0)
        up = dot(rows[...], wu[:, cols], 1, 0)
        sig = jax.nn.sigmoid(gate)
        if f == 0:
            lax.fori_loop(0, features // 256, flip, 0)
        for off in offs:
            frm = lax.rem(me + groups - off, groups)
            pull(dsend.at[f, span(frm)], drows.at[f, span(frm)],
                 d_ssem.at[f, off], d_rsem.at[f, off], {"expert": frm})
        grad = drows[f].astype(F32)
        delta_g[:, cols] = (grad * up * sig * (1.0 + gate * (1.0 - sig))).astype(BF)
        delta_u[:, cols] = (grad * gate * sig).astype(BF)

    def weight_block(mask, f):
        cols = slice(f * tile, (f + 1) * tile)
        start = pl.multiple_of(peer_dp(mask) * block, block)
        x = xt[pl.ds(start, block), :]
        return dot(x, delta_g[:, cols], 1, 0), dot(x, delta_u[:, cols], 1, 0)

    def core_stage(f):
        for mask in range(ways - 1, 0, -2):
            place = mask >> 1
            gate, up = weight_block(mask, f)
            core_send[f, place, :, 0:tile] = gate.astype(BF)
            core_send[f, place, :, tile:] = up.astype(BF)
            push(core_send.at[f, place], core_recv.at[f, place],
                 c_ssem.at[f, place], c_rsem.at[f, place], {"dp": peer_dp(1)})

    def hop(f, which, bit, mask, value):
        at = index[which, bit, mask ^ (1 << bit)]
        hop_send[f, at] = value.astype(BF)
        push(hop_send.at[f, at], hop_recv.at[f, at], h_ssem.at[f, at], h_rsem.at[f, at],
             {"dp": peer_dp(1 << bit)})

    def arrived(f, which, bit, mask):
        at = index[which, bit, mask]
        pull(hop_send.at[f, at], hop_recv.at[f, at], h_ssem.at[f, at], h_rsem.at[f, at],
             {"dp": peer_dp(1 << bit)})
        return hop_recv[f, at].astype(F32)

    def first_hops(f):
        for mask in range(ways - 2, -1, -2):
            place = mask >> 1
            pull(core_send.at[f, place], core_recv.at[f, place],
                 c_ssem.at[f, place], c_rsem.at[f, place], {"dp": peer_dp(1)})
            parts = weight_block(mask, f)
            for which in range(2):
                other = core_recv[f, place, :, which * tile : (which + 1) * tile]
                part = parts[which] + other.astype(F32)
                bit = orders[which][1]
                if mask >> bit & 1:
                    hop(f, which, bit, mask, part)
                else:
                    acc[f, which, place] = part

    def later_hops(f):
        for level in range(2, bits):
            for mask in range(ways - 2, -1, -2):
                for which in range(2):
                    order = orders[which]
                    if mask & sum(1 << b for b in order[:level]):
                        continue
                    value = acc[f, which, mask >> 1] + arrived(f, which, order[level - 1], mask)
                    if mask >> order[level] & 1:
                        hop(f, which, order[level], mask, value)
                    else:
                        acc[f, which, mask >> 1] = value

    parts = 2
    width = features // parts

    def backward(d, carry):
        cols = pl.ds(pl.multiple_of(d * 256, 256), 256)
        back[:, cols] = (
            dot(delta_g[...], wg[cols, :], 1, 1) + dot(delta_u[...], wu[cols, :], 1, 1)
        ).astype(BF)
        return carry

    def give_back():
        each = width // 256
        for part in range(parts):
            lax.fori_loop(part * each, (part + 1) * each, backward, 0)
            cols = pl.ds(part * width, width)
            for off in offs:
                to = lax.rem(me + off, groups)
                push(back.at[span(to), cols], ret.at[span(me), cols],
                     b_ssem.at[part, off], b_rsem.at[part, off], {"expert": to})

    for f in range(slices):
        deltas(f)
        if f == slices - 1:
            give_back()
        core_stage(f)
        first_hops(f)
        if f > 0:
            later_hops(f - 1)
    later_hops(slices - 1)

    for f in range(slices):
        cols = slice(f * tile, (f + 1) * tile)
        out_gate[:, cols] = acc[f, 0, 0] + arrived(f, 0, orders[0][-1], 0)
        out_up[:, cols] = acc[f, 1, 0] + arrived(f, 1, orders[1][-1], 0)
    ret[span(me), :] = back[span(me), :]
    for part in range(parts):
        cols = pl.ds(part * width, width)
        for off in offs:
            frm = lax.rem(me + groups - off, groups)
            pull(back.at[span(frm), cols], ret.at[span(frm), cols],
                 b_ssem.at[part, off], b_rsem.at[part, off], {"expert": frm})
        for c in range(part * width, (part + 1) * width, step):
            out_tok[:, c : c + step] = dot(pick[...], ret[:, c : c + step], 0, 0).astype(BF)

    for copy in started:
        copy.wait_send()


def settle(*refs):
    srcs, dsts, bufs = refs[0:3], refs[3:6], refs[6:9]
    in_sem, out_sem = refs[9:]
    ins = [pltpu.make_async_copy(s, b, in_sem.at[i]) for i, (s, b) in enumerate(zip(srcs, bufs))]
    outs = [pltpu.make_async_copy(b, d, out_sem.at[i]) for i, (b, d) in enumerate(zip(bufs, dsts))]
    for copy in ins:
        copy.start()
    for first, second in zip(ins, outs):
        first.wait()
        second.start()
    for copy in outs:
        copy.wait()


def per_device(tokens, routes, grad_hidden, w_gate, w_up):
    tok_rows, features = tokens.shape
    per_token = routes.shape[1]
    hidden = w_gate.shape[2]
    groups = lax.axis_size("expert")
    ways = lax.axis_size("dp")
    pair_count = tok_rows * per_token
    cold_most = pair_count // groups
    cold_floor = cold_most - 2 - cold_most // 8
    hot_total = pair_count - (groups - 3) * cold_floor - cold_most
    hot_most = (hot_total + 1) // 2 + min((hot_total - 2 * cold_most - 2) // 2, cold_most // 4)
    cap = (max(hot_most, cold_most) + 15) // 16 * 16
    slots = groups * cap
    block = features // ways
    bits = ways.bit_length() - 1
    hops = len(rs_plan(bits)[1])
    tile = 256
    slices = hidden // tile
    half = ways // 2
    vmem = pl.BlockSpec(memory_space=pltpu.VMEM)
    hbm = pl.BlockSpec(memory_space=pl.ANY)
    dma = pltpu.SemaphoreType.DMA
    tok_grad, gate_grad, up_grad = pl.pallas_call(
        functools.partial(kernel, groups, ways, cap, tile),
        out_shape=(
            jax.ShapeDtypeStruct((tok_rows, features), BF),
            jax.ShapeDtypeStruct((block, hidden), F32),
            jax.ShapeDtypeStruct((block, hidden), F32),
        ),
        in_specs=[vmem, vmem, vmem, vmem, hbm, hbm],
        out_specs=(vmem, vmem, vmem),
        scratch_shapes=[
            pltpu.VMEM((features, hidden), BF),
            pltpu.VMEM((features, hidden), BF),
            pltpu.VMEM((slots, tok_rows), BF),
            pltpu.VMEM((slots, features), BF),
            pltpu.VMEM((slots, features), BF),
            pltpu.VMEM((features, slots), BF),
            pltpu.VMEM((slices, slots, tile), BF),
            pltpu.VMEM((slices, slots, tile), BF),
            pltpu.VMEM((slots, hidden), BF),
            pltpu.VMEM((slots, hidden), BF),
            pltpu.VMEM((slots, features), BF),
            pltpu.VMEM((slots, features), BF),
            pltpu.VMEM((slices, half, block, 2 * tile), BF),
            pltpu.VMEM((slices, half, block, 2 * tile), BF),
            pltpu.VMEM((slices, hops, block, tile), BF),
            pltpu.VMEM((slices, hops, block, tile), BF),
            pltpu.VMEM((slices, 2, half, block, tile), F32),
            dma((2,)),
            dma((groups,)),
            dma((groups,)),
            dma((slices, groups)),
            dma((slices, groups)),
            dma((2, groups)),
            dma((2, groups)),
            dma((slices, half)),
            dma((slices, half)),
            dma((slices, hops)),
            dma((slices, hops)),
        ],
        compiler_params=pltpu.CompilerParams(collective_id=0, has_side_effects=True),
    )(tokens, routes.T, grad_hidden[:, 0], grad_hidden[:, 1], w_gate[0], w_up[0])
    results = (tok_grad, gate_grad, up_grad)
    tok_grad, gate_grad, up_grad = pl.pallas_call(
        settle,
        out_shape=tuple(jax.ShapeDtypeStruct(r.shape, r.dtype) for r in results),
        in_specs=[hbm] * 3,
        out_specs=(hbm,) * 3,
        scratch_shapes=[pltpu.VMEM(r.shape, r.dtype) for r in results] + [dma((3,)), dma((3,))],
    )(*results)
    return tok_grad, gate_grad[None], up_grad[None]


def solution(mesh):
    placed = (
        P(("dp", "expert"), None),
        P(("dp", "expert"), None),
        P(("dp", "expert"), None, None),
        P("expert", None, None),
        P("expert", None, None),
    )
    return jax.shard_map(
        per_device,
        mesh=mesh,
        in_specs=placed,
        out_specs=(P(("dp", "expert"), None), P("expert", "dp", None), P("expert", "dp", None)),
        check_vma=False,
    )
```

time: 90 us -> 93.3 us (1.037)
  Pallas kernels: 81.6 us -> 89.6 us
  local copies, waits for them, and re-layouts: 7.48 us -> 2.62 us
    pallas_call x1 -> x2, Pallas kernels: 81.6 us -> 89.6 us  [the longest x1 87.1 us: per_device(): pl.pallas_call(functools.partial(kernel, groups, ways, cap, tile), out_sh...]
    unnamed x5 -> x0, local copies, waits for them, and re-layouts: 4.9 us -> none
where the time goes in v2:
time: 93.3 us; the launch traced here: 92.9 us
  Pallas kernels  89.6 us (96%)
  local copies, waits for them, and re-layouts  2.62 us (3%)
    pallas_call x1, Pallas kernels, per_device(): pl.pallas_call(functools.partial(kernel, groups, ways, cap, tile), out_sh...  87.1 us
    pallas_call x1, Pallas kernels, per_device(): pl.pallas_call(settle, out_shape=tuple((jax.ShapeDtypeStruct(r.shape, r.d...  2.48 us

profile of v2, /device:TPU:10, one launch (start us, length us, event | category | flops | bytes accessed | tf_op | source)
XLA Modules:
  0.0 92.9 jit_solution(12752056211842324183)
XLA Ops:
  0.6 1.8 %fusion = (bf16[128,1,768]{2,1,0:T(2,128)(2,1)S(1)}, bf16[128,1,768]{2,1,0:T(2,128)(2,1)S(1)}) fusion(bf16[128,2,768]{2,1,0:T(2,128)(2,1)} %param.7), kind=kLoop, calls=%fused_computation.2 | loop fusion | bytes 786432 | tf_op jit(solution)/shard_map/slice | solution.py:345
  2.5 0.8 copy_bitcast_fusion
  3.3 87.1 %shard_map.76 = (bf16[128,2048]{1,0:T(8,128)(2,1)}, f32[256,768]{1,0:T(8,128)}, f32[256,768]{1,0:T(8,128)}) custom-call(bf16[128,2048]{1,0:T(8,128)(2,1)} %tok_ref.1, s32[2,128]{1,0:T(2,128)} %bitcast.11, bf16[128,768]{1,0:T(8,128)(2,1)} %get-tuple-element.18.gh0_ref, bf16[128,768]{1,0:T(8,128)(2,1)} %get-tuple-element.17.gh1_ref, ...), custom_call_target="tpu_custom_call" | custom-call | tf_op jit(solution)/shard_map/pallas_call | solution.py:305
  90.4 2.5 %shard_map.77 = (bf16[128,2048]{1,0:T(8,128)(2,1)}, f32[256,768]{1,0:T(8,128)}, f32[256,768]{1,0:T(8,128)}) custom-call(bf16[128,2048]{1,0:T(8,128)(2,1)} %get-tuple-element.9.refs_0_, f32[256,768]{1,0:T(8,128)} %get-tuple-element.10.refs_1_, f32[256,768]{1,0:T(8,128)} %get-tuple-element.11.refs_2_), custom_call_target="tpu_custom_call" | custom-call | tf_op jit(solution)/shard_map/pallas_call | solution.py:347
